TPU v7x, 256 devices: a whole 4x4x8 slice. The times are simulated.
256 devices in a mesh: team: 8 (over x, core), row: 2 (over z_hi), col: 16 (over y, z_lo).
Axes of the slice: x: 4, y: 4, z: 8 (z_hi: 2, z_lo: 4; z = z_hi * 4 + z_lo), core: 2. Of those that a mesh axis runs over, the one named last changes fastest.
Arguments:
- old_tiles: bfloat16 [8, 768, 256, 256], P('team', ('row', 'col')), may hold values from -4 to 4
- remap: int32 [8, 768], P('team', ('row', 'col')), may hold values from 0 to 255, as said below
- pivot_cols: bfloat16 [8, 5120, 1024], P('team', ('row', 'col')), may hold values from -6 to 6
- pivot_order: int32 [8, 2, 512], P('team'), may hold values from 0 to 511, each once within a row
- pivot_pattern: int32 [8, 2, 256], P('team'), may hold values 0 or 1
- block_inverses: float32 [8, 2, 3, 256], P('team'), may hold values from -0.05 to 0.05
- delays: int32 [8, 2], P('team'), may hold values from 0 to 128
Outputs:
- parent: float32 [2, 2048, 4096], P('row', 'team', 'col')
- second_panel: float32 [8, 5120, 512], P('team', ('row', 'col'))
Inputs may be any that keep to these rules, and one draw needn't show every extreme that they name: `remap`: tiles that one device holds go to at most 12 distinct owners, the owner of tile (i, j) being the device at row i // 8, column j; at most 2 of one device's tiles go to one owner, and in every front some owner receives exactly 2 tiles from every device.
All inputs are finite; a program needn't handle non-finite values. No bound on the sum of `pivot_pattern` on one device may be relied on, other than what follows from the above.
Results may differ from a plain program's by a relative error of at most 0.0003.
Values may be sent and summed in bfloat16 or wider, within the bound.
A program may use at most 128 MiB of HBM per device.

v0:
```python
import jax
import jax.numpy as jnp
from jax import lax
from jax.sharding import Mesh
from jax.sharding import PartitionSpec as P

COL = ("col_0", "col_1")
ROW_COL = ("row", "col_0", "col_1")


def laid_out(pieces, dim):
    shape = list(pieces.shape[1:])
    shape[dim] *= pieces.shape[0]
    return jnp.moveaxis(pieces, 0, dim).reshape(shape)


def all_blocks(shard, axes, sequence):
    pieces = shard[None]
    for k in sequence:
        pieces = lax.all_gather(pieces, axes[k], axis=0, tiled=True)
    current = [lax.axis_size(axes[k]) for k in reversed(sequence)]
    pieces = pieces.reshape(*current, *shard.shape)
    turned = sorted(range(len(sequence)), key=lambda place: sequence[len(sequence) - 1 - place])
    return pieces.transpose(*turned, *range(len(sequence), pieces.ndim)).reshape(-1, *shard.shape)


def gather_axes(shard, axes, sequence, dim):
    return laid_out(all_blocks(shard, axes, sequence), dim)


def in_blocks(shard, dim, peers):
    before, after = (shard.shape[:dim], shard.shape[dim + 1 :])
    return jnp.moveaxis(shard.reshape(*before, peers, -1, *after), dim, 0)


def summed_on_arrival(shard, axis, dim):
    pieces = in_blocks(shard, dim, lax.axis_size(axis))
    arrived = lax.all_to_all(pieces, axis, split_axis=0, concat_axis=0, tiled=True)
    return arrived.sum(axis=0)


def make_coeffs(inverses, pattern, delay, panel):
    half_panel = panel // 2
    positions = jnp.arange(panel, dtype=jnp.int32)
    active = (positions < panel - delay).astype(jnp.float32)
    active_lo = active[:half_panel]
    active_hi = active[half_panel:]
    diag_one = inverses[0] * active_lo
    off_diag = inverses[1] * pattern.astype(jnp.float32) * active_lo * active_hi
    diag_two = inverses[2] * active_hi
    return (diag_one, off_diag, diag_two)


def scale_pivots(columns, coeffs):
    diag_one, off_diag, diag_two = coeffs
    half_panel = diag_one.shape[0]
    left_half = columns[:, :half_panel]
    right_half = columns[:, half_panel:]
    return jnp.concatenate(
        [
            left_half * diag_one + right_half * off_diag,
            left_half * off_diag + right_half * diag_two,
        ],
        axis=1,
    )


def outer_update(left_rows, right_rows):
    return lax.dot_general(
        left_rows,
        right_rows,
        (((1,), (1,)), ((), ())),
        precision=lax.Precision.HIGHEST,
        preferred_element_type=jnp.float32,
    )


def local(old_tiles, remap, pivot_cols, pivot_order, pivot_pattern, block_inverses, delays):
    row_devices = lax.axis_size("row")
    col_devices = lax.axis_size(COL)
    peers = row_devices * col_devices
    row_index = lax.axis_index("row")
    col_index = lax.axis_index(COL)
    held = old_tiles.shape[1]
    tile_side = old_tiles.shape[2]
    panel = pivot_order.shape[2]
    rows_here = pivot_cols.shape[1]
    front_order = rows_here * peers
    contrib = front_order - 2 * panel
    tile_count = contrib // tile_side
    row_span = contrib // row_devices
    col_span = contrib // col_devices
    per_row = row_span // tile_side
    per_col = col_span // tile_side
    old_flat = old_tiles[0].reshape(held, tile_side * tile_side)
    targets = remap[0]
    tile_row = targets // tile_count
    tile_col = targets % tile_count
    owners = tile_row // per_row * col_devices + tile_col // per_col
    slots = tile_row % per_row * per_col + tile_col % per_col
    spread = min(peers, held // 2)
    capacity = (held + spread - 1) // spread
    indices = jnp.arange(held, dtype=jnp.int32)
    matched = (owners[:, None] == owners[None, :]) & (indices[None, :] < indices[:, None])
    ranks = jnp.sum(matched.astype(jnp.int32), axis=1)
    positions = owners * capacity + ranks
    places = peers * capacity
    routing = jnp.arange(places, dtype=jnp.int32)[:, None] == positions[None, :]
    outgoing = jnp.dot(
        routing.astype(jnp.bfloat16), old_flat, preferred_element_type=jnp.float32
    ).astype(jnp.bfloat16)
    labels = jnp.sum(jnp.where(routing, slots[None, :] + 1, 0), axis=1) - 1
    arrived, arrived_tags = (
        lax.all_to_all(outgoing, ROW_COL, split_axis=0, concat_axis=0, tiled=True),
        lax.all_to_all(labels, ROW_COL, split_axis=0, concat_axis=0, tiled=True),
    )
    slots_here = per_row * per_col
    collect = (jnp.arange(slots_here, dtype=jnp.int32)[:, None] == arrived_tags[None, :]).astype(
        jnp.bfloat16
    )
    summed = jnp.dot(collect, arrived, preferred_element_type=jnp.float32)
    front_c = (
        summed.reshape(per_row, per_col, tile_side, tile_side)
        .transpose(0, 2, 1, 3)
        .reshape(row_span, col_span)
    )
    orders = pivot_order[0]
    coeff_one = make_coeffs(block_inverses[0, 0], pivot_pattern[0, 0], delays[0, 0], panel)
    coeff_two = make_coeffs(block_inverses[0, 1], pivot_pattern[0, 1], delays[0, 1], panel)
    own_rows = pivot_cols[0]
    own_first = jnp.take(own_rows[:, :panel], orders[0], axis=1)
    own_second_raw = jnp.take(own_rows[:, panel:], orders[1], axis=1)
    own_start = (row_index * col_devices + col_index) * rows_here
    both_panels = gather_axes(
        jnp.concatenate([own_first, own_second_raw], axis=1), ROW_COL, (0, 2, 1), 0
    )
    first = both_panels[:, :panel].astype(jnp.float32)
    picked = jnp.take(first, panel + orders[1], axis=0)
    second = both_panels[:, panel:].astype(jnp.float32) - outer_update(
        scale_pivots(first, coeff_one), picked
    )
    own_second = lax.dynamic_slice_in_dim(second, own_start, rows_here, 0)
    pivot_span = 2 * panel
    row_first = scale_pivots(
        lax.dynamic_slice_in_dim(first, pivot_span + row_index * row_span, row_span, 0), coeff_one
    )
    row_second = scale_pivots(
        lax.dynamic_slice_in_dim(second, pivot_span + row_index * row_span, row_span, 0), coeff_two
    )
    col_first = lax.dynamic_slice_in_dim(first, pivot_span + col_index * col_span, col_span, 0)
    col_second = lax.dynamic_slice_in_dim(second, pivot_span + col_index * col_span, col_span, 0)
    parent = summed_on_arrival(
        front_c - outer_update(row_first, col_first) - outer_update(row_second, col_second),
        "team",
        0,
    )
    return (parent[None], own_second[None])


def solution(mesh):
    torus = Mesh(
        mesh.devices.reshape(mesh.shape["team"], mesh.shape["row"], 4, 4),
        ("team", "row", "col_0", "col_1"),
    )
    in_specs = (
        P("team", ROW_COL, None, None),
        P("team", ROW_COL),
        P("team", ROW_COL, None),
        P("team", None, None),
        P("team", None, None),
        P("team", None, None, None),
        P("team", None),
    )
    out_specs = (P("row", "team", COL), P("team", ROW_COL, None))
    return jax.shard_map(local, mesh=torus, in_specs=in_specs, out_specs=out_specs, check_vma=False)
```

profile of v0, /device:TPU:48, one launch (start us, length us, event | category | flops | bytes accessed | tf_op | source)
XLA Modules:
  0.0 439.0 jit_solution(3782700567953836906)
XLA Ops:
  7.2 0.0 all-gather.4.cloned.1.call-start
  7.2 0.8 fusion.45
  8.0 1.2 copy.18
  9.2 0.0 copy-start.8
  9.3 2.6 gather_fusion.2
  11.8 0.0 copy-start.3
  11.8 1.9 select_bitcast_fusion
  13.8 2.6 gather_fusion.1
  16.4 1.1 select_bitcast_fusion.1
  17.5 1.8 pad_maximum_fusion
  19.3 1.9 copy.19
  21.2 23.7 %all-gather = bf16[320,1024]{1,0:T(8,128)(2,1)} all-gather(bf16[160,1024]{1,0:T(8,128)(2,1)} %copy.19), channel_id=2, replica_groups=mesh['team'=8,'row'=2,'col_0'=4,'col_1'=4] {'row'}, dimensions={0}, use_global_device_ids=true | all-gather | bytes 983040 | tf_op jit(solution)/shard_map/all_gather | solution.py:20
  44.9 0.0 all-gather.4.cloned.1.call-update
  44.9 0.0 copy-done.8
  45.0 0.2 convert_reduce_fusion
  45.2 0.1 select_reduce_fusion
  45.3 0.7 sub.44
  46.0 8.4 %all-to-all-start = ((s32[32,2,1]{1,2,0:T(1,128)}), s32[32,2,1]{1,2,0:T(1,128)S(1)}, u32[]{:S(2)}, u32[]{:S(2)}) async-start(s32[32,2,1]{1,2,0:T(1,128)} %bitcast.5), calls=%async_computation | async-start | bytes 32768 | tf_op jit(solution)/shard_map/all_to_all | solution.py:115
  54.4 0.0 copy-done.3
  54.4 1.8 copy.21
  56.2 5.7 %convolution_convert_fusion = bf16[64,65536]{1,0:T(8,128)(2,1)} fusion(bf16[24,65536]{1,0:T(8,128)(2,1)S(1)} %bitcast.64, s32[24]{0:T(128)S(1)} %fusion.37), kind=kOutput, calls=%fused_computation.3 | convolution fusion | flops 205522432 | bytes 11534432 | tf_op jit(solution)/shard_map/dot_general | solution.py:109
  61.9 10.6 %all_to_all.16 = bf16[32,2,65536]{2,1,0:T(2,128)(2,1)} reshape(bf16[64,65536]{1,0:T(8,128)(2,1)} %convolution_convert_fusion) | data formatting | bytes 16777216 | tf_op jit(solution)/shard_map/all_to_all | solution.py:114
  72.5 0.0 copy-start.7
  72.5 0.0 all-to-all-done
  72.6 10.0 %all-to-all-start.1 = ((bf16[32,2,65536]{2,1,0:T(2,128)(2,1)}), bf16[32,2,65536]{2,1,0:T(2,128)(2,1)}, u32[]{:S(2)}, u32[]{:S(2)}) async-start(bf16[32,2,65536]{2,1,0:T(2,128)(2,1)} %all_to_all.16), calls=%async_computation.1 | async-start | bytes 16777216 | tf_op jit(solution)/shard_map/all_to_all | solution.py:114
  82.6 0.2 all-gather.6.cloned.1.call-start
  82.8 73.6 %all-gather.4.cloned.1.call-done = bf16[8,160,1024]{2,1,0:T(8,128)(2,1)} async-done(((bf16[2,160,1024]{2,1,0:T(8,128)(2,1)}), bf16[8,160,1024]{2,1,0:T(8,128)(2,1)}) %all-gather.4.cloned.1.call-update) | async-done | bytes 2621456 | tf_op jit(solution)/shard_map/all_gather | solution.py:20
  156.4 0.0 all-gather.6.cloned.1.call-update
  156.5 0.0 copy-done.7
  156.5 0.6 fusion.46
  158.4 0.0 copy-done.4
  158.4 0.0 copy-done.6
  158.4 0.0 copy-done.5
  158.5 0.5 broadcast.309
  159.0 0.7 reduce.3
  159.7 0.1 eq.58
  159.8 132.2 %all-to-all-done.1 = bf16[32,2,65536]{2,1,0:T(2,128)(2,1)} async-done(((bf16[32,2,65536]{2,1,0:T(2,128)(2,1)}), bf16[32,2,65536]{2,1,0:T(2,128)(2,1)}, u32[]{:S(2)}, u32[]{:S(2)}) %all-to-all-start.1) | async-done | bytes 8388640 | tf_op jit(solution)/shard_map/all_to_all | solution.py:114
  292.0 10.3 %all_to_all.18 = bf16[64,65536]{1,0:T(8,128)(2,1)} reshape(bf16[32,2,65536]{2,1,0:T(2,128)(2,1)} %all-to-all-done.1) | data formatting | bytes 16777216 | tf_op jit(solution)/shard_map/all_to_all | solution.py:114
  302.3 4.6 %fusion.27 = f32[8,65536]{1,0:T(8,128)S(1)} fusion(bf16[64,65536]{1,0:T(8,128)(2,1)} %all_to_all.18, s32[64]{0:T(128)S(1)} %eq.58), kind=kOutput, calls=%fused_computation.48 | convolution fusion | flops 67109376 | bytes 10486016 | tf_op jit(solution)/shard_map/dot_general | solution.py:121
  306.9 1.6 reshape_transpose_reshape.3
  308.5 18.0 %all-gather.6.cloned.1.call-done = bf16[32,160,1024]{2,1,0:T(8,128)(2,1)} async-done(((bf16[8,160,1024]{2,1,0:T(8,128)(2,1)}), bf16[32,160,1024]{2,1,0:T(8,128)(2,1)}) %all-gather.6.cloned.1.call-update) | async-done | bytes 10485776 | tf_op jit(solution)/shard_map/all_gather | solution.py:20
  326.5 9.8 %copy.20 = bf16[2,4,4,160,1024]{4,3,2,1,0:T(8,128)(2,1)} copy(bf16[2,4,4,160,1024]{4,3,0,2,1:T(8,128)(2,1)} %bitcast.65) | data formatting | bytes 20971520 | tf_op jit(solution)/shard_map/transpose | solution.py:24
  336.3 10.0 %fusion.42 = (bf16[5120,512]{1,0:T(8,128)(2,1)}, f32[5120,512]{1,0:T(8,128)}) fusion(bf16[5120,1024]{1,0:T(8,128)(2,1)} %bitcast.60), kind=kLoop, calls=%fused_computation.99 | loop fusion | flops 2621440 | bytes 20971520 | tf_op jit(solution)/shard_map/slice | solution.py:137
  346.3 6.2 %gather_fusion = f32[512,512]{1,0:T(8,128)S(1)} fusion(f32[5120,512]{1,0:T(8,128)} %get-tuple-element.12, s32[1024]{0:T(1024)S(1)} %pad_clamp_fusion), kind=kCustom, calls=%fused_computation.2 | custom fusion | bytes 2099200 | tf_op jit(solution)/shard_map/jit(_take)/gather | solution.py:138
  352.5 0.0 slice-start.1
  352.5 0.0 slice-start.2
  352.5 9.2 %multiply_add_fusion.1 = (f32[5120,256]{1,0:T(8,128)}, f32[5120,256]{1,0:T(8,128)}) fusion(f32[5120,512]{1,0:T(8,128)} %get-tuple-element.12, f32[256]{0:T(256)S(1)} %get-tuple-element.32, f32[256]{0:T(256)S(1)} %get-tuple-element.30, f32[256]{0:T(256)S(1)} %get-tuple-element.31), kind=kLoop, calls=%fused_computation.10 | loop fusion | flops 7864320 | bytes 20974592 | tf_op jit(solution)/shard_map/add | solution.py:61
  361.7 2.8 multiply_add_fusion.5
  364.5 0.0 slice-done
  364.5 0.0 slice-done.1
  364.5 0.0 slice-done.2
  364.5 0.9 copy-done.1
  365.4 20.4 %convert_subtract_fusion = f32[5120,512]{1,0:T(8,128)S(1)} fusion(f32[5120,256]{1,0:T(8,128)} %get-tuple-element.8, f32[5120,256]{1,0:T(8,128)S(1)} %copy-done.1, bf16[5120,1024]{1,0:T(8,128)(2,1)S(1)} %bitcast.63, f32[512,512]{1,0:T(8,128)S(1)} %gather_fusion, pred[512]{0:T(512)(128)(4,1)S(1)} %get-tuple-element.28), kind=kOutput, calls=%fused_computation.8 | convolution fusion | flops 16114253824 | bytes 27263488 | tf_op jit(solution)/shard_map/dot_general | solution.py:69
  385.8 0.0 copy-start
  385.8 0.0 copy-start.2
  385.8 0.6 multiply_add_fusion.3
  386.4 2.6 copy-done.2
  389.0 3.4 fusion.17
  392.4 0.0 copy-done
  392.4 5.0 %fusion.14 = f32[2048,256]{1,0:T(8,128)} fusion(f32[2048,256]{1,0:T(8,128)S(1)} %fusion.17, f32[2048,256]{1,0:T(8,128)S(1)} %get-tuple-element.6, f32[2048,256]{1,0:T(8,128)S(1)} %get-tuple-element.5, f32[5120,512]{1,0:T(8,128)S(1)} %convert_subtract_fusion, s32[]{:T(128)S(6)} %select_n.109), kind=kOutput, calls=%fused_computation.19 | convolution fusion | flops 3222798336 | bytes 8912900 | tf_op jit(solution)/shard_map/dot_general | solution.py:69
  397.4 6.8 %all-to-all-start.2 = ((f32[8,256,256]{2,1,0:T(8,128)}), f32[8,256,256]{2,1,0:T(8,128)S(1)}, u32[]{:S(2)}, u32[]{:S(2)}) async-start(f32[8,256,256]{2,1,0:T(8,128)} %bitcast.28), calls=%async_computation.2 | async-start | bytes 4194304 | tf_op jit(solution)/shard_map/all_to_all | solution.py:38
  404.2 1.7 dynamic-slice_bitcast_fusion
  405.9 25.5 %all-to-all-done.2 = f32[8,256,256]{2,1,0:T(8,128)S(1)} async-done(((f32[8,256,256]{2,1,0:T(8,128)}), f32[8,256,256]{2,1,0:T(8,128)S(1)}, u32[]{:S(2)}, u32[]{:S(2)}) %all-to-all-start.2) | async-done | bytes 2097184 | tf_op jit(solution)/shard_map/all_to_all | solution.py:38
  431.3 0.8 reduce_sum.32
  (24 shorter events, 0.2 us)
Async XLA Ops:
  7.2 149.3 %all-gather.4.cloned.1.call-start = ((), (), s32[]{:S(2)}) async-start(), calls=%async_computation.3 | async-start | bytes 3276800 | tf_op jit(solution)/shard_map/all_gather | solution.py:20
  9.2 35.7 %copy-start.8 = (s32[1,24]{1,0:T(1,128)S(1)}, s32[1,24]{1,0:T(1,128)}, u32[]{:S(2)}) copy-start(s32[1,24]{1,0:T(1,128)} %param.10) | copy-start | bytes 292
  11.8 42.6 %copy-start.3 = (bf16[1,24,256,256]{3,2,1,0:T(8,128)(2,1)S(1)}, bf16[1,24,256,256]{3,2,1,0:T(8,128)(2,1)}, u32[]{:S(2)}) copy-start(bf16[1,24,256,256]{3,2,1,0:T(8,128)(2,1)} %param.9) | copy-start | bytes 9437188
  46.0 26.5 %all-to-all-start = ((s32[32,2,1]{1,2,0:T(1,128)}), s32[32,2,1]{1,2,0:T(1,128)S(1)}, u32[]{:S(2)}, u32[]{:S(2)}) async-start(s32[32,2,1]{1,2,0:T(1,128)} %bitcast.5), calls=%async_computation | async-start | bytes 32768 | tf_op jit(solution)/shard_map/all_to_all | solution.py:115
  72.5 83.9 %copy-start.7 = (s32[1,2]{1,0:T(1,128)S(1)}, s32[1,2]{1,0:T(1,128)}, u32[]{:S(2)}) copy-start(s32[1,2]{1,0:T(1,128)} %param.15) | copy-start | bytes 28
  72.5 85.8 %copy-start.4 = (s32[1,2,512]{2,1,0:T(2,128)S(1)}, s32[1,2,512]{2,1,0:T(2,128)}, u32[]{:S(2)}) copy-start(s32[1,2,512]{2,1,0:T(2,128)} %param.12) | copy-start | bytes 12292
  72.5 85.9 %copy-start.6 = (s32[1,2,256]{2,1,0:T(2,128)S(1)}, s32[1,2,256]{2,1,0:T(2,128)}, u32[]{:S(2)}) copy-start(s32[1,2,256]{2,1,0:T(2,128)} %param.13) | copy-start | bytes 6148
  72.5 85.9 %copy-start.5 = (f32[1,2,3,256]{3,1,2,0:T(2,128)S(1)}, f32[1,2,3,256]{3,1,2,0:T(2,128)}, u32[]{:S(2)}) copy-start(f32[1,2,3,256]{3,1,2,0:T(2,128)} %param.14) | copy-start | bytes 18436
  72.6 219.4 %all-to-all-start.1 = ((bf16[32,2,65536]{2,1,0:T(2,128)(2,1)}), bf16[32,2,65536]{2,1,0:T(2,128)(2,1)}, u32[]{:S(2)}, u32[]{:S(2)}) async-start(bf16[32,2,65536]{2,1,0:T(2,128)(2,1)} %all_to_all.16), calls=%async_computation.1 | async-start | bytes 16777216 | tf_op jit(solution)/shard_map/all_to_all | solution.py:114
  82.6 243.9 %all-gather.6.cloned.1.call-start = ((), (), s32[]{:S(2)}) async-start(), calls=%async_computation.4 | async-start | bytes 13107200 | tf_op jit(solution)/shard_map/all_gather | solution.py:20
  346.3 18.2 %slice-start = ((s8[10485760]{0:T(1024)(128)(4,1)}), s8[2097152]{0:T(1024)(128)(4,1)S(1)}, s32[]{:S(2)}) async-start(s8[10485760]{0:T(1024)(128)(4,1)} %bitcast.61), calls=%async_computation.5 | async-start | bytes 4194304
  352.5 12.0 %slice-start.1 = ((s8[10485760]{0:T(1024)(128)(4,1)}), s8[4194304]{0:T(1024)(128)(4,1)S(1)}, s32[]{:S(2)}) async-start(s8[10485760]{0:T(1024)(128)(4,1)} %bitcast.61), calls=%async_computation.6 | async-start | bytes 8388608
  352.5 12.0 %slice-start.2 = ((s8[10485760]{0:T(1024)(128)(4,1)}), s8[4194304]{0:T(1024)(128)(4,1)S(1)}, s32[]{:S(2)}) async-start(s8[10485760]{0:T(1024)(128)(4,1)} %bitcast.61), calls=%async_computation.7 | async-start | bytes 8388608
  361.6 3.7 copy-start.1
  385.8 6.6 %copy-start = (f32[5120,512]{1,0:T(8,128)}, f32[5120,512]{1,0:T(8,128)S(1)}, u32[]{:S(2)}) copy-start(f32[5120,512]{1,0:T(8,128)S(1)} %convert_subtract_fusion) | copy-start | bytes 31457284
  385.8 3.2 copy-start.2
  397.4 34.0 %all-to-all-start.2 = ((f32[8,256,256]{2,1,0:T(8,128)}), f32[8,256,256]{2,1,0:T(8,128)S(1)}, u32[]{:S(2)}, u32[]{:S(2)}) async-start(f32[8,256,256]{2,1,0:T(8,128)} %bitcast.28), calls=%async_computation.2 | async-start | bytes 4194304 | tf_op jit(solution)/shard_map/all_to_all | solution.py:38
Sparse Core Ops, SparseCore 0:
  45.0 111.3 all-gather.3
  158.2 168.2 all-gather.5
where the time goes:
time: 440 us; the launch traced here: 439 us
  waiting for transfers between devices  249 us (57%)
  local copies, waits for them, and re-layouts  56.5 us (13%)
  matrix products  39.1 us (9%)
  other arithmetic  29.3 us (7%)
  starting transfers between devices  25.5 us (6%)
  blocking collectives  23.7 us (5%)
  between operations  15.7 us (4%)
    all_to_all x1, waiting for transfers between devices, local(): lax.all_to_all(outgoing, ROW_COL, split_axis=0, concat_axis=0, tiled=True)  132 us
    all_gather x2, waiting for transfers between devices, all_blocks(): pieces = lax.all_gather(pieces, axes[k], axis=0, tiled=True)  91.6 us
    dot_general x3, matrix products, outer_update(): lax.dot_general(left_rows, right_rows, (((1,), (1,)), ((), ())), precisio...  28.8 us
    all_to_all x1, waiting for transfers between devices, summed_on_arrival(): lax.all_to_all(pieces, axis, split_axis=0, concat_axis=0, tiled=True)  25.5 us
    all_gather x1, blocking collectives, all_blocks(): pieces = lax.all_gather(pieces, axes[k], axis=0, tiled=True)  23.7 us
    all_to_all x2, local copies, waits for them, and re-layouts, local(): lax.all_to_all(outgoing, ROW_COL, split_axis=0, concat_axis=0, tiled=True)  20.9 us
    add x3, other arithmetic, scale_pivots(): left_half * diag_one + right_half * off_diag  12.5 us
    all_to_all x1, starting transfers between devices, local(): lax.all_to_all(outgoing, ROW_COL, split_axis=0, concat_axis=0, tiled=True)  10 us
  transfers between devices with their start and end apart: 5, of which 4 were waited for; matrix products, arithmetic and copies ran while one was open for 4% of the time, Pallas kernels for 0%

commit v1 on v0

--- a/solution.py
+++ b/solution.py
@@ -17,7 +17,9 @@
 def all_blocks(shard, axes, sequence):
     pieces = shard[None]
     for k in sequence:
-        pieces = lax.all_gather(pieces, axes[k], axis=0, tiled=True)
+        pieces = jnp.concatenate(
+            lax.all_to_all(jnp.stack([pieces] * lax.axis_size(axes[k])), axes[k], 0, 0), axis=0
+        )
     current = [lax.axis_size(axes[k]) for k in reversed(sequence)]
     pieces = pieces.reshape(*current, *shard.shape)
     turned = sorted(range(len(sequence)), key=lambda place: sequence[len(sequence) - 1 - place])

time: 440 us -> 502 us (1.14); the launches traced: 439 us -> 494 us
  blocking collectives: 23.7 us -> 86.1 us
  between operations: 15.7 us -> 2.28 us
  waiting for transfers between devices: 249 us -> 240 us
  starting transfers between devices: 25.5 us -> 31.5 us
    all_to_all x0 -> x1, waiting for transfers between devices: none -> 94.4 us  [all_blocks(): lax.all_to_all(jnp.stack([pieces] * lax.axis_size(axes[k])), axes[k], 0, 0)]
    all_gather x2 -> x0, waiting for transfers between devices: 91.6 us -> none  [all_blocks(): pieces = lax.all_gather(pieces, axes[k], axis=0, tiled=True)]
    all_to_all x0 -> x2, blocking collectives: none -> 86.1 us  [all_blocks(): lax.all_to_all(jnp.stack([pieces] * lax.axis_size(axes[k])), axes[k], 0, 0)]
    all_gather x1 -> x0, blocking collectives: 23.7 us -> none  [all_blocks(): pieces = lax.all_gather(pieces, axes[k], axis=0, tiled=True)]
    all_to_all x1, waiting for transfers between devices: 132 us -> 120 us  [local(): lax.all_to_all(outgoing, ROW_COL, split_axis=0, concat_axis=0, tiled=True)]
    all_to_all x0 -> x1, starting transfers between devices: none -> 6.83 us  [all_blocks(): lax.all_to_all(jnp.stack([pieces] * lax.axis_size(axes[k])), axes[k], 0, 0)]
    another operation x0 -> x3, local copies, waits for them, and re-layouts: none -> 6.21 us  [all_blocks(): jnp.stack([pieces] * lax.axis_size(axes[k]))]
  transfers between devices with their start and end apart: 5 -> 4, of which waited for: 4 -> 3; matrix products, arithmetic and copies ran while one was open for 4% -> 17% of each run, Pallas kernels for 0% -> 0%
where the time goes in v1:
time: 502 us; the launch traced here: 494 us
  waiting for transfers between devices  240 us (48%)
  blocking collectives  86.1 us (17%)
  local copies, waits for them, and re-layouts  60.2 us (12%)
  matrix products  43.5 us (9%)
  starting transfers between devices  31.5 us (6%)
  other arithmetic  30.8 us (6%)
    all_to_all x1, waiting for transfers between devices, local(): lax.all_to_all(outgoing, ROW_COL, split_axis=0, concat_axis=0, tiled=True)  120 us
    all_to_all x1, waiting for transfers between devices, all_blocks(): lax.all_to_all(jnp.stack([pieces] * lax.axis_size(axes[k])), axes[k], 0, 0)  94.4 us
    all_to_all x2, blocking collectives, all_blocks(): lax.all_to_all(jnp.stack([pieces] * lax.axis_size(axes[k])), axes[k], 0, 0)  86.1 us
    dot_general x3, matrix products, outer_update(): lax.dot_general(left_rows, right_rows, (((1,), (1,)), ((), ())), precisio...  31.7 us
    all_to_all x1, waiting for transfers between devices, summed_on_arrival(): lax.all_to_all(pieces, axis, split_axis=0, concat_axis=0, tiled=True)  25.5 us
    all_to_all x2, local copies, waits for them, and re-layouts, local(): lax.all_to_all(outgoing, ROW_COL, split_axis=0, concat_axis=0, tiled=True)  20.8 us
    add x3, other arithmetic, scale_pivots(): left_half * diag_one + right_half * off_diag  16.6 us
    all_to_all x1, starting transfers between devices, local(): lax.all_to_all(labels, ROW_COL, split_axis=0, concat_axis=0, tiled=True)  11.1 us
  transfers between devices with their start and end apart: 4, of which 3 were waited for; matrix products, arithmetic and copies ran while one was open for 17% of the time, Pallas kernels for 0%

profile of v1, /device:TPU:48, one launch (start us, length us, event | category | flops | bytes accessed | tf_op | source)
XLA Modules:
  0.0 494.1 jit_solution(8017353610093166720)
XLA Ops:
  0.6 0.7 fusion.36
  1.3 0.7 fusion.34
  2.0 0.7 fusion.33
  2.6 0.2 convert_reduce_fusion
  2.8 0.1 select_reduce_fusion
  2.9 0.7 sub.44
  3.7 11.1 %all-to-all-start = ((s32[32,2,1]{1,2,0:T(1,128)}), s32[32,2,1]{1,2,0:T(1,128)S(1)}, u32[]{:S(2)}, u32[]{:S(2)}) async-start(s32[32,2,1]{1,2,0:T(1,128)} %bitcast.5), calls=%async_computation | async-start | bytes 32768 | tf_op jit(solution)/shard_map/all_to_all | solution.py:117
  14.8 0.8 fusion.45
  15.6 1.2 copy.19
  16.8 2.0 gather_fusion.2
  18.8 0.1 select_bitcast_fusion
  18.9 2.0 gather_fusion.1
  20.9 0.1 select_bitcast_fusion.1
  21.1 0.1 maximum_bitcast_fusion
  21.2 0.2 pad_maximum_fusion
  21.4 0.5 copy.20
  21.8 0.0 all-to-all-done
  21.8 25.3 %all_to_all.38 = bf16[2,1,160,1024]{3,2,1,0:T(8,128)(2,1)S(1)} all-to-all(bf16[2,1,160,1024]{3,2,1,0:T(8,128)(2,1)S(1)} %copy.20), channel_id=1, replica_groups=mesh['team'=8,'row'=2,'col_0'=4,'col_1'=4] {'row'}, dimensions={0} | all-to-all | bytes 1310720 | tf_op jit(solution)/shard_map/all_to_all | solution.py:21
  47.1 0.3 stack.10
  47.4 60.9 %all_to_all.39 = bf16[4,2,160,1024]{3,2,1,0:T(8,128)(2,1)S(1)} all-to-all(bf16[4,2,160,1024]{3,2,1,0:T(8,128)(2,1)S(1)} %stack.10), channel_id=1, replica_groups=mesh['team'=8,'row'=2,'col_0'=4,'col_1'=4] {'col_1'}, dimensions={0} | all-to-all | bytes 5242880 | tf_op jit(solution)/shard_map/all_to_all | solution.py:21
  108.3 5.4 %stack.11 = bf16[4,8,160,1024]{3,2,1,0:T(8,128)(2,1)} broadcast(bf16[8,160,1024]{2,1,0:T(8,128)(2,1)S(1)} %bitcast.68), dimensions={1,2,3} | broadcast | bytes 13107200 | tf_op jit(solution)/shard_map/stack | solution.py:21
  113.7 0.0 copy-start.3
  113.7 6.8 %all-to-all-start.4 = ((bf16[4,8,160,1024]{3,2,1,0:T(8,128)(2,1)}), bf16[4,8,160,1024]{3,2,1,0:T(8,128)(2,1)}, u32[]{:S(2)}, u32[]{:S(2)}) async-start(bf16[4,8,160,1024]{3,2,1,0:T(8,128)(2,1)} %stack.11), calls=%async_computation.4 | async-start | bytes 20971520 | tf_op jit(solution)/shard_map/all_to_all | solution.py:21
  120.6 0.0 copy-done.3
  120.6 1.8 copy.22
  122.3 5.8 %convolution_convert_fusion = bf16[64,65536]{1,0:T(8,128)(2,1)} fusion(bf16[24,65536]{1,0:T(8,128)(2,1)S(1)} %bitcast.67, s32[24]{0:T(128)S(1)} %fusion.37), kind=kOutput, calls=%fused_computation.3 | convolution fusion | flops 205522432 | bytes 11534432 | tf_op jit(solution)/shard_map/dot_general | solution.py:111
  128.2 10.6 %all_to_all.25 = bf16[32,2,65536]{2,1,0:T(2,128)(2,1)} reshape(bf16[64,65536]{1,0:T(8,128)(2,1)} %convolution_convert_fusion) | data formatting | bytes 16777216 | tf_op jit(solution)/shard_map/all_to_all | solution.py:116
  138.7 94.4 %all-to-all-done.4 = bf16[4,8,160,1024]{3,2,1,0:T(8,128)(2,1)} async-done(((bf16[4,8,160,1024]{3,2,1,0:T(8,128)(2,1)}), bf16[4,8,160,1024]{3,2,1,0:T(8,128)(2,1)}, u32[]{:S(2)}, u32[]{:S(2)}) %all-to-all-start.4) | async-done | bytes 10485792 | tf_op jit(solution)/shard_map/all_to_all | solution.py:21
  233.1 9.2 %all-to-all-start.1 = ((bf16[32,2,65536]{2,1,0:T(2,128)(2,1)}), bf16[32,2,65536]{2,1,0:T(2,128)(2,1)}, u32[]{:S(2)}, u32[]{:S(2)}) async-start(bf16[32,2,65536]{2,1,0:T(2,128)(2,1)} %all_to_all.25), calls=%async_computation.1 | async-start | bytes 16777216 | tf_op jit(solution)/shard_map/all_to_all | solution.py:116
  242.3 0.0 copy-done.7
  242.4 0.6 fusion.46
  244.3 0.0 copy-done.4
  244.3 0.0 copy-done.6
  244.3 0.0 copy-done.5
  244.4 0.5 broadcast.311
  244.9 0.7 reduce.3
  245.6 0.1 eq.58
  245.7 10.0 %copy.21 = bf16[2,4,4,160,1024]{4,3,2,1,0:T(8,128)(2,1)} copy(bf16[2,4,4,160,1024]{4,3,0,2,1:T(8,128)(2,1)} %bitcast.15) | data formatting | bytes 20971520 | tf_op jit(solution)/shard_map/transpose | solution.py:26
  255.7 9.7 %fusion.42 = (bf16[5120,512]{1,0:T(8,128)(2,1)}, f32[5120,512]{1,0:T(8,128)}) fusion(bf16[5120,1024]{1,0:T(8,128)(2,1)} %bitcast.63), kind=kLoop, calls=%fused_computation.100 | loop fusion | flops 2621440 | bytes 20971520 | tf_op jit(solution)/shard_map/slice | solution.py:139
  265.5 6.0 %gather_fusion = f32[512,512]{1,0:T(8,128)S(1)} fusion(f32[5120,512]{1,0:T(8,128)} %get-tuple-element.12, s32[1024]{0:T(1024)S(1)} %pad_clamp_fusion), kind=kCustom, calls=%fused_computation.2 | custom fusion | bytes 2099200 | tf_op jit(solution)/shard_map/jit(_take)/gather | solution.py:140
  271.5 0.0 slice-start
  271.5 4.8 multiply_add_fusion.5
  276.3 9.3 %multiply_add_fusion.1 = (f32[5120,256]{1,0:T(8,128)}, f32[5120,256]{1,0:T(8,128)}) fusion(f32[5120,512]{1,0:T(8,128)} %get-tuple-element.12, f32[256]{0:T(256)S(1)} %get-tuple-element.32, f32[256]{0:T(256)S(1)} %get-tuple-element.30, f32[256]{0:T(256)S(1)} %get-tuple-element.31), kind=kLoop, calls=%fused_computation.10 | loop fusion | flops 7864320 | bytes 20974592 | tf_op jit(solution)/shard_map/add | solution.py:63
  285.5 0.0 slice-done
  285.5 0.0 slice-done.1
  285.5 0.0 slice-done.2
  285.6 21.1 %convert_subtract_fusion = f32[5120,512]{1,0:T(8,128)S(1)} fusion(f32[5120,256]{1,0:T(8,128)} %get-tuple-element.8, f32[5120,256]{1,0:T(8,128)} %get-tuple-element.7, bf16[5120,1024]{1,0:T(8,128)(2,1)S(1)} %bitcast.66, f32[512,512]{1,0:T(8,128)S(1)} %gather_fusion, pred[512]{0:T(512)(128)(4,1)S(1)} %get-tuple-element.28), kind=kOutput, calls=%fused_computation.8 | convolution fusion | flops 16114253824 | bytes 27263488 | tf_op jit(solution)/shard_map/dot_general | solution.py:71
  306.7 0.0 copy-start
  306.7 4.0 copy-done
  310.7 2.5 multiply_add_fusion.3
  313.3 119.9 %all-to-all-done.1 = bf16[32,2,65536]{2,1,0:T(2,128)(2,1)} async-done(((bf16[32,2,65536]{2,1,0:T(2,128)(2,1)}), bf16[32,2,65536]{2,1,0:T(2,128)(2,1)}, u32[]{:S(2)}, u32[]{:S(2)}) %all-to-all-start.1) | async-done | bytes 8388640 | tf_op jit(solution)/shard_map/all_to_all | solution.py:116
  433.1 10.2 %all_to_all.27 = bf16[64,65536]{1,0:T(8,128)(2,1)} reshape(bf16[32,2,65536]{2,1,0:T(2,128)(2,1)} %all-to-all-done.1) | data formatting | bytes 16777216 | tf_op jit(solution)/shard_map/all_to_all | solution.py:116
  443.3 6.0 %fusion.27 = f32[8,65536]{1,0:T(8,128)} fusion(bf16[64,65536]{1,0:T(8,128)(2,1)} %all_to_all.27, s32[64]{0:T(128)S(1)} %eq.58), kind=kOutput, calls=%fused_computation.49 | convolution fusion | flops 67109376 | bytes 10486016 | tf_op jit(solution)/shard_map/dot_general | solution.py:123
  449.3 1.9 reshape_transpose_reshape.3
  451.2 0.0 copy-start.1
  451.2 0.0 copy-start.2
  451.2 4.6 fusion.17
  455.8 0.0 copy-done.1
  455.8 0.0 copy-done.2
  455.8 6.0 %fusion.14 = f32[2048,256]{1,0:T(8,128)} fusion(f32[2048,256]{1,0:T(8,128)S(1)} %fusion.17, f32[2048,256]{1,0:T(8,128)S(1)} %copy-done.2, f32[2048,256]{1,0:T(8,128)S(1)} %copy-done.1, f32[5120,512]{1,0:T(8,128)} %copy-done, s32[]{:T(128)S(6)} %select_n.109), kind=kOutput, calls=%fused_computation.19 | convolution fusion | flops 3222798336 | bytes 8912900 | tf_op jit(solution)/shard_map/dot_general | solution.py:71
  461.8 4.3 all-to-all-start.5
  466.1 1.7 dynamic-slice_bitcast_fusion
  467.8 25.5 %all-to-all-done.5 = f32[8,256,256]{2,1,0:T(8,128)S(1)} async-done(((f32[8,256,256]{2,1,0:T(8,128)}), f32[8,256,256]{2,1,0:T(8,128)S(1)}, u32[]{:S(2)}, u32[]{:S(2)}) %all-to-all-start.5) | async-done | bytes 2097184 | tf_op jit(solution)/shard_map/all_to_all | solution.py:40
  493.2 0.8 reduce_sum.32
  (22 shorter events, 0.1 us)
Async XLA Ops:
  3.7 18.2 %all-to-all-start = ((s32[32,2,1]{1,2,0:T(1,128)}), s32[32,2,1]{1,2,0:T(1,128)S(1)}, u32[]{:S(2)}, u32[]{:S(2)}) async-start(s32[32,2,1]{1,2,0:T(1,128)} %bitcast.5), calls=%async_computation | async-start | bytes 32768 | tf_op jit(solution)/shard_map/all_to_all | solution.py:117
  113.7 6.8 %copy-start.3 = (bf16[1,24,256,256]{3,2,1,0:T(8,128)(2,1)S(1)}, bf16[1,24,256,256]{3,2,1,0:T(8,128)(2,1)}, u32[]{:S(2)}) copy-start(bf16[1,24,256,256]{3,2,1,0:T(8,128)(2,1)} %param.9) | copy-start | bytes 9437188
  113.7 119.4 %all-to-all-start.4 = ((bf16[4,8,160,1024]{3,2,1,0:T(8,128)(2,1)}), bf16[4,8,160,1024]{3,2,1,0:T(8,128)(2,1)}, u32[]{:S(2)}, u32[]{:S(2)}) async-start(bf16[4,8,160,1024]{3,2,1,0:T(8,128)(2,1)} %stack.11), calls=%async_computation.4 | async-start | bytes 20971520 | tf_op jit(solution)/shard_map/all_to_all | solution.py:21
  138.7 103.6 %copy-start.7 = (s32[1,2]{1,0:T(1,128)S(1)}, s32[1,2]{1,0:T(1,128)}, u32[]{:S(2)}) copy-start(s32[1,2]{1,0:T(1,128)} %param.15) | copy-start | bytes 28
  138.7 105.6 %copy-start.4 = (s32[1,2,512]{2,1,0:T(2,128)S(1)}, s32[1,2,512]{2,1,0:T(2,128)}, u32[]{:S(2)}) copy-start(s32[1,2,512]{2,1,0:T(2,128)} %param.12) | copy-start | bytes 12292
  138.7 105.6 %copy-start.6 = (s32[1,2,256]{2,1,0:T(2,128)S(1)}, s32[1,2,256]{2,1,0:T(2,128)}, u32[]{:S(2)}) copy-start(s32[1,2,256]{2,1,0:T(2,128)} %param.13) | copy-start | bytes 6148
  138.7 105.6 %copy-start.5 = (f32[1,2,3,256]{3,1,2,0:T(2,128)S(1)}, f32[1,2,3,256]{3,1,2,0:T(2,128)}, u32[]{:S(2)}) copy-start(f32[1,2,3,256]{3,1,2,0:T(2,128)} %param.14) | copy-start | bytes 18436
  233.1 200.0 %all-to-all-start.1 = ((bf16[32,2,65536]{2,1,0:T(2,128)(2,1)}), bf16[32,2,65536]{2,1,0:T(2,128)(2,1)}, u32[]{:S(2)}, u32[]{:S(2)}) async-start(bf16[32,2,65536]{2,1,0:T(2,128)(2,1)} %all_to_all.25), calls=%async_computation.1 | async-start | bytes 16777216 | tf_op jit(solution)/shard_map/all_to_all | solution.py:116
  271.5 14.1 %slice-start = ((s8[10485760]{0:T(1024)(128)(4,1)}), s8[4194304]{0:T(1024)(128)(4,1)S(1)}, s32[]{:S(2)}) async-start(s8[10485760]{0:T(1024)(128)(4,1)} %bitcast.64), calls=%async_computation.6 | async-start | bytes 8388608
  276.3 9.3 %slice-start.1 = ((s8[10485760]{0:T(1024)(128)(4,1)}), s8[4194304]{0:T(1024)(128)(4,1)S(1)}, s32[]{:S(2)}) async-start(s8[10485760]{0:T(1024)(128)(4,1)} %bitcast.64), calls=%async_computation.7 | async-start | bytes 8388608
  276.3 9.3 %slice-start.2 = ((s8[10485760]{0:T(1024)(128)(4,1)}), s8[2097152]{0:T(1024)(128)(4,1)S(1)}, s32[]{:S(2)}) async-start(s8[10485760]{0:T(1024)(128)(4,1)} %bitcast.64), calls=%async_computation.8 | async-start | bytes 4194304
  306.7 4.0 copy-start
  451.2 4.6 copy-start.1
  451.2 4.6 copy-start.2
  461.8 31.5 %all-to-all-start.5 = ((f32[8,256,256]{2,1,0:T(8,128)}), f32[8,256,256]{2,1,0:T(8,128)S(1)}, u32[]{:S(2)}, u32[]{:S(2)}) async-start(f32[8,256,256]{2,1,0:T(8,128)} %bitcast.30), calls=%async_computation.5 | async-start | bytes 4194304 | tf_op jit(solution)/shard_map/all_to_all | solution.py:40
